TPU v7x, 32 devices: a whole 2x2x4 slice. The times are simulated.
32 devices in a mesh: row: 4 (over y, core), col: 8 (over z, x).
Axes of the slice: x: 2, y: 2, z: 4, core: 2. Of those that a mesh axis runs over, the one named last changes fastest.
Arguments:
- obs_cell: int32 [32, 16, 32, 128], P(('row', 'col')), may hold values from 0 to 8388607, as said below
- obs_value: bfloat16 [32, 16, 32, 128], P(('row', 'col')), may hold values from -6 to 6
- obs_weight: bfloat16 [32, 16, 32, 128], P(('row', 'col')), may hold values from 0.5 to 2
- obs_count: int32 [32, 16, 32], P(('row', 'col')), may hold values from 0 to 128, as said below
- kappa_field: float32 [2048, 4096], P('row', 'col'), may hold values from 0.2 to 6
Outputs:
- solution_field: float32 [2048, 4096], P('row', 'col')
- residual: float32 [2048, 4096], P('row', 'col')
Inputs may be any that keep to these rules, and one draw needn't show every extreme that they name: `obs_cell`: block (s, t, d) holds observations for tile t of device d, where device d is number d // 8 along row and d % (8) along col, and tile t is number t // 4 among the device's tiles along rows and t % (4) along columns, each tile 128 by 128 cells; every slot of the block, padding included, names a cell of that tile as row * 4096 + column. Slots at positions obs_count and beyond are padding. For one owner device, chosen afresh in each draw, every block from every source and tile is full.
All inputs are finite; a program needn't handle non-finite values.
Results may differ from a plain program's by a relative error of at most 0.0029.
Values may be sent and summed in bfloat16 or wider, within the bound.
A program may use at most 64 MiB of HBM per device.

v0:
```python
from functools import partial
import jax
import jax.numpy as jnp
from jax import lax
from jax.sharding import PartitionSpec as P

TILE = 128
ITERS = 3
smooth_weight = 0.05


def extended(block, sides, width):
    for axis, dim in sides:
        count = lax.axis_size(axis)
        forward = [(i, i + 1) for i in range(count - 1)]
        backward = [(target, source) for source, target in forward]
        low = lax.ppermute(
            lax.slice_in_dim(block, block.shape[dim] - width, None, axis=dim), axis, forward
        )
        high = lax.ppermute(lax.slice_in_dim(block, 0, width, axis=dim), axis, backward)
        block = jnp.concatenate([low, block, high], axis=dim)
    return block


def stencil_step(padded, kappa_field):
    center = padded[1:-1, 1:-1]
    beside = padded[2:, 1:-1] + padded[:-2, 1:-1]
    beside = beside + padded[1:-1, 2:] + padded[1:-1, :-2]
    return (4.0 + kappa_field) * center - beside


def bin_tile(members, cols_all):
    cell_ids, obs_vals, obs_wts, is_live = members
    local_row = cell_ids // cols_all % TILE
    local_col = cell_ids % cols_all % TILE
    offsets = jnp.arange(TILE, dtype=jnp.int32)
    row_onehot = (local_row[:, None] == offsets[None, :]).astype(jnp.bfloat16)
    col_onehot = (local_col[:, None] == offsets[None, :]).astype(jnp.bfloat16)
    zero_fill = jnp.zeros_like(obs_wts)
    masked_weight = jnp.where(is_live, obs_wts, zero_fill)
    product = (obs_wts.astype(jnp.float32) * obs_vals.astype(jnp.float32)).astype(jnp.bfloat16)
    masked_resp = jnp.where(is_live, product, zero_fill)
    stacked = jnp.concatenate(
        [col_onehot * masked_weight[:, None], col_onehot * masked_resp[:, None]], axis=1
    )
    return lax.dot_general(
        row_onehot, stacked, (((0,), (0,)), ((), ())), preferred_element_type=jnp.float32
    )


def per_device(obs_cell, obs_value, obs_weight, obs_count, kappa_field):
    rows_dev, cols_dev = kappa_field.shape
    cols_all = cols_dev * lax.axis_size("col")
    tiles_dev = obs_cell.shape[1]
    block_rows = obs_cell.shape[3]
    got_cells, got_counts = (
        lax.all_to_all(obs_cell, ("row", "col"), split_axis=2, concat_axis=2, tiled=True),
        lax.all_to_all(obs_count, ("row", "col"), split_axis=2, concat_axis=2, tiled=True),
    )
    got_values, got_weights = (
        lax.all_to_all(obs_value, ("row", "col"), split_axis=2, concat_axis=2, tiled=True),
        lax.all_to_all(obs_weight, ("row", "col"), split_axis=2, concat_axis=2, tiled=True),
    )
    flat_rows = obs_cell.shape[2] * block_rows
    positions = jnp.arange(block_rows, dtype=jnp.int32)
    is_live = (positions[None, None, :] < got_counts.reshape(tiles_dev, -1)[:, :, None]).reshape(
        tiles_dev, flat_rows
    )
    members = (
        got_cells.reshape(tiles_dev, flat_rows),
        got_values.reshape(tiles_dev, flat_rows),
        got_weights.reshape(tiles_dev, flat_rows),
        is_live,
    )
    binned = lax.map(partial(bin_tile, cols_all=cols_all), members)
    tile_rows = rows_dev // TILE
    tile_cols = cols_dev // TILE
    binned = (
        binned.reshape(tile_rows, tile_cols, TILE, 2, TILE)
        .transpose(3, 0, 2, 1, 4)
        .reshape(2, rows_dev, cols_dev)
    )
    weight_field = binned[0]
    response = binned[1]

    def operate(field):
        first = extended(field, (("row", 0), ("col", 1)), 1)
        inner = stencil_step(first, kappa_field)
        second = extended(inner, (("row", 0), ("col", 1)), 1)
        return weight_field * field + smooth_weight * stencil_step(second, kappa_field)

    solution_field = jnp.zeros_like(response)
    residual = response

    def two_products(current, image):
        return lax.psum((jnp.sum(current * current), jnp.sum(current * image)), ("row", "col"))

    image = operate(residual)
    norm_now, curvature = two_products(residual, image)
    alpha = norm_now / curvature
    direction, along = (residual, image)
    for step in range(ITERS):
        solution_field = solution_field + alpha * direction
        residual = residual - alpha * along
        if step + 1 < ITERS:
            image = operate(residual)
            norm_next, curvature = two_products(residual, image)
            ratio = norm_next / norm_now
            alpha = norm_next / (curvature - ratio * norm_next / alpha)
            direction = residual + ratio * direction
            along = image + ratio * along
            norm_now = norm_next
    return (solution_field, residual)


def solution(mesh):
    placed = (
        P(("row", "col"), None, None, None),
        P(("row", "col"), None, None, None),
        P(("row", "col"), None, None, None),
        P(("row", "col"), None, None),
        P("row", "col"),
    )
    return jax.shard_map(
        per_device,
        mesh=mesh,
        in_specs=placed,
        out_specs=(P("row", "col"), P("row", "col")),
        check_vma=False,
    )
```

profile of v0, /device:TPU:0, one launch (start us, length us, event | category | flops | bytes accessed | tf_op | source)
XLA Modules:
  0.0 424.5 jit_solution(13311932666679719868)
XLA Ops:
  2.0 7.3 %all-to-all-start.1 = ((s32[1,16,32]{1,0,2:T(1,128)}), s32[1,16,32]{1,0,2:T(1,128)S(1)}, u32[]{:S(2)}, u32[]{:S(2)}) async-start(s32[1,16,32]{1,0,2:T(1,128)} %copy.16), calls=%async_computation.1 | async-start | bytes 32768 | tf_op jit(solution)/shard_map/all_to_all | solution.py:58
  9.3 1.6 copy.20
  11.0 5.5 %all-to-all-done.1 = s32[1,16,32]{1,0,2:T(1,128)S(1)} async-done(((s32[1,16,32]{1,0,2:T(1,128)}), s32[1,16,32]{1,0,2:T(1,128)S(1)}, u32[]{:S(2)}, u32[]{:S(2)}) %all-to-all-start.1) | async-done | bytes 2080 | tf_op jit(solution)/shard_map/all_to_all | solution.py:58
  16.4 2.6 all-to-all-start.3
  20.6 1.8 copy.14
  22.5 4.3 %all-to-all-done.3 = bf16[1,16,32,128]{3,1,0,2:T(8,128)(2,1)S(1)} async-done(((bf16[1,16,32,128]{3,1,0,2:T(8,128)(2,1)}), bf16[1,16,32,128]{3,1,0,2:T(8,128)(2,1)S(1)}, u32[]{:S(2)}, u32[]{:S(2)}) %all-to-all-start.3) | async-done | bytes 131104 | tf_op jit(solution)/shard_map/all_to_all | solution.py:61
  26.8 2.6 all-to-all-start.2
  30.3 6.8 %all-to-all-done.2 = bf16[1,16,32,128]{3,1,0,2:T(8,128)(2,1)S(1)} async-done(((bf16[1,16,32,128]{3,1,0,2:T(8,128)(2,1)}), bf16[1,16,32,128]{3,1,0,2:T(8,128)(2,1)S(1)}, u32[]{:S(2)}, u32[]{:S(2)}) %all-to-all-start.2) | async-done | bytes 131104 | tf_op jit(solution)/shard_map/all_to_all | solution.py:62
  37.2 2.6 all-to-all-start
  40.6 9.7 %all-to-all-done = s32[1,16,32,128]{3,1,0,2:T(8,128)S(1)} async-done(((s32[1,16,32,128]{3,1,0,2:T(8,128)}), s32[1,16,32,128]{3,1,0,2:T(8,128)S(1)}, u32[]{:S(2)}, u32[]{:S(2)}) %all-to-all-start) | async-done | bytes 262176 | tf_op jit(solution)/shard_map/all_to_all | solution.py:57
  50.5 83.1 %while.13 = (s32[]{:T(128)}, f32[16,128,256]{2,1,0:T(8,128)S(1)}, s32[16,4096]{1,0:T(8,128)S(1)}, pred[16,4096]{1,0:T(8,128)(4,1)}, bf16[16,4096]{1,0:T(8,128)(2,1)}, /*index=5*/bf16[16,4096]{1,0:T(8,128)(2,1)S(1)}, s32[]{:T(128)}) while((s32[]{:T(128)}, f32[16,128,256]{2,1,0:T(8,128)S(1)}, s32[16,4096]{1,0:T(8,128)S(1)}, ...), condition=%wide.region_1.2_spmd, body=%wide.region_0.1_spmd.sunk | while | flops 274919424 | bytes 4550757 | solution.py:75
  52.3 1.9 fusion.62
  57.5 1.9 fusion.62
  62.7 1.9 fusion.62
  67.9 1.9 fusion.62
  73.1 1.9 fusion.62
  78.3 1.9 fusion.62
  83.5 1.9 fusion.62
  88.7 1.9 fusion.62
  93.9 1.9 fusion.62
  99.0 1.9 fusion.62
  104.2 1.9 fusion.62
  109.4 1.9 fusion.62
  114.6 1.9 fusion.62
  119.8 1.9 fusion.62
  125.0 1.9 fusion.62
  130.2 1.9 fusion.62
  134.9 2.3 reshape.137
  139.8 2.1 collective-permute-start.1
  143.3 2.0 collective-permute-done
  146.7 4.6 %collective-permute-start.3 = (f32[514,1]{1,0:T(8,128)S(1)}, f32[514,1]{1,0:T(8,128)S(1)}, u32[]{:S(2)}, u32[]{:S(2)}) collective-permute-start(f32[514,1]{1,0:T(8,128)S(1)} %get-tuple-element.158), channel_id=1, source_target_pairs={{0,1},{1,2},{2,3},{3,4},{4,5},{5,6},{6,7},{8,9},{9,10},{10,11},{11... | collective-permute-start | bytes 6176 | tf_op jit(solution)/shard_map/ppermute | solution.py:17
  151.2 3.9 collective-permute-done.2
  155.2 6.6 %collective-permute-done.3 = f32[514,1]{1,0:T(8,128)S(1)} collective-permute-done((f32[514,1]{1,0:T(8,128)S(1)}, f32[514,1]{1,0:T(8,128)S(1)}, u32[]{:S(2)}, u32[]{:S(2)}) %collective-permute-start.3) | collective-permute-done | bytes 2088 | tf_op jit(solution)/shard_map/ppermute | solution.py:17
  162.5 2.2 collective-permute-start.5
  166.1 1.7 collective-permute-done.4
  169.3 4.8 %collective-permute-start.7 = (f32[514,1]{1,0:T(8,128)S(1)}, f32[514,1]{1,0:T(8,128)S(1)}, u32[]{:S(2)}, u32[]{:S(2)}) collective-permute-start(f32[514,1]{1,0:T(8,128)S(1)} %get-tuple-element.156), channel_id=1, source_target_pairs={{0,1},{1,2},{2,3},{3,4},{4,5},{5,6},{6,7},{8,9},{9,10},{10,11},{11... | collective-permute-start | bytes 6176 | tf_op jit(solution)/shard_map/ppermute | solution.py:17
  174.1 4.1 collective-permute-done.6
  178.2 7.2 %collective-permute-done.7 = f32[514,1]{1,0:T(8,128)S(1)} collective-permute-done((f32[514,1]{1,0:T(8,128)S(1)}, f32[514,1]{1,0:T(8,128)S(1)}, u32[]{:S(2)}, u32[]{:S(2)}) %collective-permute-start.7) | collective-permute-done | bytes 2088 | tf_op jit(solution)/shard_map/ppermute | solution.py:17
  185.4 2.6 multiply_reduce_fusion.4
  188.0 39.1 %all-reduce.2 = (f32[]{:T(128)}, f32[]{:T(128)}) all-reduce(f32[]{:T(128)} %get-tuple-element.144, f32[]{:T(128)} %get-tuple-element.134), channel_id=1, replica_groups=mesh['row'=4,'col'=8] {'row','col'}, use_global_device_ids=true, to_apply=%region_3.4 | all-reduce | flops 2 | bytes 16 | tf_op jit(solution)/shard_map/psum | solution.py:96
  232.4 4.5 %collective-permute-done.8 = f32[1,512]{1,0:T(1,128)S(1)} collective-permute-done((f32[1,512]{1,0:T(1,128)S(1)}, f32[1,512]{1,0:T(1,128)S(1)}, u32[]{:S(2)}, u32[]{:S(2)}) %collective-permute-start.8) | collective-permute-done | bytes 2080 | tf_op jit(solution)/shard_map/ppermute | solution.py:20
  238.4 4.7 %collective-permute-start.11 = (f32[514,1]{1,0:T(8,128)S(1)}, f32[514,1]{1,0:T(8,128)S(1)}, u32[]{:S(2)}, u32[]{:S(2)}) collective-permute-start(f32[514,1]{1,0:T(8,128)S(1)} %get-tuple-element.154), channel_id=1, source_target_pairs={{0,1},{1,2},{2,3},{3,4},{4,5},{5,6},{6,7},{8,9},{9,10},{10,11},{11... | collective-permute-start | bytes 6176 | tf_op jit(solution)/shard_map/ppermute | solution.py:17
  243.1 3.7 collective-permute-done.10
  246.8 7.3 %collective-permute-done.11 = f32[514,1]{1,0:T(8,128)S(1)} collective-permute-done((f32[514,1]{1,0:T(8,128)S(1)}, f32[514,1]{1,0:T(8,128)S(1)}, u32[]{:S(2)}, u32[]{:S(2)}) %collective-permute-start.11) | collective-permute-done | bytes 2088 | tf_op jit(solution)/shard_map/ppermute | solution.py:17
  254.9 2.2 collective-permute-start.13
  258.4 1.7 collective-permute-done.12
  261.6 5.0 %collective-permute-start.15 = (f32[514,1]{1,0:T(8,128)S(1)}, f32[514,1]{1,0:T(8,128)S(1)}, u32[]{:S(2)}, u32[]{:S(2)}) collective-permute-start(f32[514,1]{1,0:T(8,128)S(1)} %get-tuple-element.152), channel_id=1, source_target_pairs={{0,1},{1,2},{2,3},{3,4},{4,5},{5,6},{6,7},{8,9},{9,10},{10,11},{11... | collective-permute-start | bytes 6176 | tf_op jit(solution)/shard_map/ppermute | solution.py:17
  266.6 3.9 collective-permute-done.14
  270.6 7.2 %collective-permute-done.15 = f32[514,1]{1,0:T(8,128)S(1)} collective-permute-done((f32[514,1]{1,0:T(8,128)S(1)}, f32[514,1]{1,0:T(8,128)S(1)}, u32[]{:S(2)}, u32[]{:S(2)}) %collective-permute-start.15) | collective-permute-done | bytes 2088 | tf_op jit(solution)/shard_map/ppermute | solution.py:17
  277.8 2.6 multiply_reduce_fusion.2
  280.4 40.2 %all-reduce.1 = (f32[]{:T(128)}, f32[]{:T(128)}) all-reduce(f32[]{:T(128)} %get-tuple-element.113, f32[]{:T(128)} %get-tuple-element.112), channel_id=1, replica_groups=mesh['row'=4,'col'=8] {'row','col'}, use_global_device_ids=true, to_apply=%region_7.8 | all-reduce | flops 2 | bytes 16 | tf_op jit(solution)/shard_map/psum | solution.py:96
  325.0 1.9 multiply_subtract_fusion.1
  329.5 4.5 %collective-permute-done.16 = f32[1,512]{1,0:T(1,128)S(1)} collective-permute-done((f32[1,512]{1,0:T(1,128)S(1)}, f32[1,512]{1,0:T(1,128)S(1)}, u32[]{:S(2)}, u32[]{:S(2)}) %collective-permute-start.16) | collective-permute-done | bytes 2080 | tf_op jit(solution)/shard_map/ppermute | solution.py:20
  335.5 4.7 %collective-permute-start.19 = (f32[514,1]{1,0:T(8,128)S(1)}, f32[514,1]{1,0:T(8,128)S(1)}, u32[]{:S(2)}, u32[]{:S(2)}) collective-permute-start(f32[514,1]{1,0:T(8,128)S(1)} %get-tuple-element.150), channel_id=1, source_target_pairs={{0,1},{1,2},{2,3},{3,4},{4,5},{5,6},{6,7},{8,9},{9,10},{10,11},{11... | collective-permute-start | bytes 6176 | tf_op jit(solution)/shard_map/ppermute | solution.py:17
  340.2 3.7 collective-permute-done.18
  343.9 7.3 %collective-permute-done.19 = f32[514,1]{1,0:T(8,128)S(1)} collective-permute-done((f32[514,1]{1,0:T(8,128)S(1)}, f32[514,1]{1,0:T(8,128)S(1)}, u32[]{:S(2)}, u32[]{:S(2)}) %collective-permute-start.19) | collective-permute-done | bytes 2088 | tf_op jit(solution)/shard_map/ppermute | solution.py:17
  352.0 2.2 collective-permute-start.21
  355.5 1.7 collective-permute-done.20
  358.7 4.8 %collective-permute-start.23 = (f32[514,1]{1,0:T(8,128)S(1)}, f32[514,1]{1,0:T(8,128)S(1)}, u32[]{:S(2)}, u32[]{:S(2)}) collective-permute-start(f32[514,1]{1,0:T(8,128)S(1)} %get-tuple-element.148), channel_id=1, source_target_pairs={{0,1},{1,2},{2,3},{3,4},{4,5},{5,6},{6,7},{8,9},{9,10},{10,11},{11... | collective-permute-start | bytes 6176 | tf_op jit(solution)/shard_map/ppermute | solution.py:17
  363.5 4.1 collective-permute-done.22
  367.6 7.2 %collective-permute-done.23 = f32[514,1]{1,0:T(8,128)S(1)} collective-permute-done((f32[514,1]{1,0:T(8,128)S(1)}, f32[514,1]{1,0:T(8,128)S(1)}, u32[]{:S(2)}, u32[]{:S(2)}) %collective-permute-start.23) | collective-permute-done | bytes 2088 | tf_op jit(solution)/shard_map/ppermute | solution.py:17
  374.9 2.6 multiply_reduce_fusion
  377.5 39.0 %all-reduce = (f32[]{:T(128)}, f32[]{:T(128)}) all-reduce(f32[]{:T(128)} %get-tuple-element.111, f32[]{:T(128)} %get-tuple-element.110), channel_id=1, replica_groups=mesh['row'=4,'col'=8] {'row','col'}, use_global_device_ids=true, to_apply=%region_11.12 | all-reduce | flops 2 | bytes 16 | tf_op jit(solution)/shard_map/psum | solution.py:96
  420.3 4.3 %multiply_subtract_fusion = (f32[512,512]{1,0:T(8,128)}, f32[512,512]{1,0:T(8,128)}) fusion(f32[512,512]{1,0:T(8,128)S(1)} %multiply_subtract_fusion.1, f32[512,512]{1,0:T(8,128)} %get-tuple-element.132, f32[]{:T(128)S(6)} %div.37, f32[]{:T(128)S(6)} %div.39, f32[512,512]{1,0:T(8,128)} %get-tuple-element.133, f32[512,512]{1,0:T(8,128)} %get-tuple-element.135, ...), kind=kLoop, calls=%fused_computation.118 | loop fusion | flops 3932160 | bytes 8388628 | tf_op jit(solution)/shard_map/sub | solution.py:104
  (159 shorter events, 83.1 us)
Async XLA Ops:
  2.0 14.4 %all-to-all-start.1 = ((s32[1,16,32]{1,0,2:T(1,128)}), s32[1,16,32]{1,0,2:T(1,128)S(1)}, u32[]{:S(2)}, u32[]{:S(2)}) async-start(s32[1,16,32]{1,0,2:T(1,128)} %copy.16), calls=%async_computation.1 | async-start | bytes 32768 | tf_op jit(solution)/shard_map/all_to_all | solution.py:58
  16.4 10.4 %all-to-all-start.3 = ((bf16[1,16,32,128]{3,1,0,2:T(8,128)(2,1)}), bf16[1,16,32,128]{3,1,0,2:T(8,128)(2,1)S(1)}, u32[]{:S(2)}, u32[]{:S(2)}) async-start(bf16[1,16,32,128]{3,1,0,2:T(8,128)(2,1)} %copy.20), calls=%async_computation.3 | async-start | bytes 262144 | tf_op jit(solution)/shard_map/all_to_all | solution.py:61
  26.8 10.4 %all-to-all-start.2 = ((bf16[1,16,32,128]{3,1,0,2:T(8,128)(2,1)}), bf16[1,16,32,128]{3,1,0,2:T(8,128)(2,1)S(1)}, u32[]{:S(2)}, u32[]{:S(2)}) async-start(bf16[1,16,32,128]{3,1,0,2:T(8,128)(2,1)} %copy.18), calls=%async_computation.2 | async-start | bytes 262144 | tf_op jit(solution)/shard_map/all_to_all | solution.py:62
  37.2 13.0 %all-to-all-start = ((s32[1,16,32,128]{3,1,0,2:T(8,128)}), s32[1,16,32,128]{3,1,0,2:T(8,128)S(1)}, u32[]{:S(2)}, u32[]{:S(2)}) async-start(s32[1,16,32,128]{3,1,0,2:T(8,128)} %copy.14), calls=%async_computation | async-start | bytes 524288 | tf_op jit(solution)/shard_map/all_to_all | solution.py:57
  133.6 1.3 copy-start.5
  139.7 45.7 %copy-start.2 = (f32[1,4,128,4,128]{4,3,2,1,0:T(4,128)}, f32[1,4,128,4,128]{4,3,2,1,0:T(4,128)S(1)}, u32[]{:S(2)}) copy-start(f32[1,4,128,4,128]{4,3,2,1,0:T(4,128)S(1)} %get-tuple-element.145) | copy-start | bytes 3145732
  139.8 88.6 %copy-start.1 = (f32[1,4,128,4,128]{4,3,2,1,0:T(4,128)}, f32[1,4,128,4,128]{4,3,2,1,0:T(4,128)S(1)}, u32[]{:S(2)}) copy-start(f32[1,4,128,4,128]{4,3,2,1,0:T(4,128)S(1)} %get-tuple-element.146) | copy-start | bytes 3145732
  139.8 22.0 %copy-start = (f32[512,512]{1,0:T(8,128)S(1)}, f32[512,512]{1,0:T(8,128)}, u32[]{:S(2)}) copy-start(f32[512,512]{1,0:T(8,128)} %param.11) | copy-start | bytes 3145732
  139.8 3.4 collective-permute-start.1
  141.9 3.3 collective-permute-start
  145.4 9.8 %collective-permute-start.2 = (f32[514,1]{1,0:T(8,128)S(1)}, f32[514,1]{1,0:T(8,128)S(1)}, u32[]{:S(2)}, u32[]{:S(2)}) collective-permute-start(f32[514,1]{1,0:T(8,128)S(1)} %get-tuple-element.157), channel_id=1, source_target_pairs={{1,0},{2,1},{3,2},{4,3},{5,4},{6,5},{7,6},{9,8},{10,9},{11,10},{12... | collective-permute-start | bytes 6176 | tf_op jit(solution)/shard_map/ppermute | solution.py:20
  146.7 15.1 %collective-permute-start.3 = (f32[514,1]{1,0:T(8,128)S(1)}, f32[514,1]{1,0:T(8,128)S(1)}, u32[]{:S(2)}, u32[]{:S(2)}) collective-permute-start(f32[514,1]{1,0:T(8,128)S(1)} %get-tuple-element.158), channel_id=1, source_target_pairs={{0,1},{1,2},{2,3},{3,4},{4,5},{5,6},{6,7},{8,9},{9,10},{10,11},{11... | collective-permute-start | bytes 6176 | tf_op jit(solution)/shard_map/ppermute | solution.py:17
  162.5 3.5 collective-permute-start.5
  164.7 3.1 collective-permute-start.4
  168.0 10.3 %collective-permute-start.6 = (f32[514,1]{1,0:T(8,128)S(1)}, f32[514,1]{1,0:T(8,128)S(1)}, u32[]{:S(2)}, u32[]{:S(2)}) collective-permute-start(f32[514,1]{1,0:T(8,128)S(1)} %get-tuple-element.155), channel_id=1, source_target_pairs={{1,0},{2,1},{3,2},{4,3},{5,4},{6,5},{7,6},{9,8},{10,9},{11,10},{12... | collective-permute-start | bytes 6176 | tf_op jit(solution)/shard_map/ppermute | solution.py:20
  169.3 16.2 %collective-permute-start.7 = (f32[514,1]{1,0:T(8,128)S(1)}, f32[514,1]{1,0:T(8,128)S(1)}, u32[]{:S(2)}, u32[]{:S(2)}) collective-permute-start(f32[514,1]{1,0:T(8,128)S(1)} %get-tuple-element.156), channel_id=1, source_target_pairs={{0,1},{1,2},{2,3},{3,4},{4,5},{5,6},{6,7},{8,9},{9,10},{10,11},{11... | collective-permute-start | bytes 6176 | tf_op jit(solution)/shard_map/ppermute | solution.py:17
  229.8 2.6 collective-permute-start.9
  231.1 5.8 %collective-permute-start.8 = (f32[1,512]{1,0:T(1,128)S(1)}, f32[1,512]{1,0:T(1,128)S(1)}, u32[]{:S(2)}, u32[]{:S(2)}) collective-permute-start(f32[1,512]{1,0:T(1,128)S(1)} %get-tuple-element.168), channel_id=1, source_target_pairs={{8,0},{16,8},{24,16},{9,1},{17,9},{25,17},{10,2},{18,10},{26,18},{... | collective-permute-start | bytes 6152 | tf_op jit(solution)/shard_map/ppermute | solution.py:20
  237.1 9.7 %collective-permute-start.10 = (f32[514,1]{1,0:T(8,128)S(1)}, f32[514,1]{1,0:T(8,128)S(1)}, u32[]{:S(2)}, u32[]{:S(2)}) collective-permute-start(f32[514,1]{1,0:T(8,128)S(1)} %get-tuple-element.153), channel_id=1, source_target_pairs={{1,0},{2,1},{3,2},{4,3},{5,4},{6,5},{7,6},{9,8},{10,9},{11,10},{12... | collective-permute-start | bytes 6176 | tf_op jit(solution)/shard_map/ppermute | solution.py:20
  238.4 39.4 %copy-start.3 = (f32[1,4,128,4,128]{4,3,2,1,0:T(4,128)S(1)}, f32[1,4,128,4,128]{4,3,2,1,0:T(4,128)}, u32[]{:S(2)}) copy-start(f32[1,4,128,4,128]{4,3,2,1,0:T(4,128)} %copy-done.2) | copy-start | bytes 3145732
  238.4 15.7 %collective-permute-start.11 = (f32[514,1]{1,0:T(8,128)S(1)}, f32[514,1]{1,0:T(8,128)S(1)}, u32[]{:S(2)}, u32[]{:S(2)}) collective-permute-start(f32[514,1]{1,0:T(8,128)S(1)} %get-tuple-element.154), channel_id=1, source_target_pairs={{0,1},{1,2},{2,3},{3,4},{4,5},{5,6},{6,7},{8,9},{9,10},{10,11},{11... | collective-permute-start | bytes 6176 | tf_op jit(solution)/shard_map/ppermute | solution.py:17
  254.9 3.5 collective-permute-start.13
  257.1 3.1 collective-permute-start.12
  260.3 10.3 %collective-permute-start.14 = (f32[514,1]{1,0:T(8,128)S(1)}, f32[514,1]{1,0:T(8,128)S(1)}, u32[]{:S(2)}, u32[]{:S(2)}) collective-permute-start(f32[514,1]{1,0:T(8,128)S(1)} %get-tuple-element.151), channel_id=1, source_target_pairs={{1,0},{2,1},{3,2},{4,3},{5,4},{6,5},{7,6},{9,8},{10,9},{11,10},{12... | collective-permute-start | bytes 6176 | tf_op jit(solution)/shard_map/ppermute | solution.py:20
  261.6 16.2 %collective-permute-start.15 = (f32[514,1]{1,0:T(8,128)S(1)}, f32[514,1]{1,0:T(8,128)S(1)}, u32[]{:S(2)}, u32[]{:S(2)}) collective-permute-start(f32[514,1]{1,0:T(8,128)S(1)} %get-tuple-element.152), channel_id=1, source_target_pairs={{0,1},{1,2},{2,3},{3,4},{4,5},{5,6},{6,7},{8,9},{9,10},{10,11},{11... | collective-permute-start | bytes 6176 | tf_op jit(solution)/shard_map/ppermute | solution.py:17
  326.9 2.6 collective-permute-start.17
  328.2 5.8 %collective-permute-start.16 = (f32[1,512]{1,0:T(1,128)S(1)}, f32[1,512]{1,0:T(1,128)S(1)}, u32[]{:S(2)}, u32[]{:S(2)}) collective-permute-start(f32[1,512]{1,0:T(1,128)S(1)} %get-tuple-element.164), channel_id=1, source_target_pairs={{8,0},{16,8},{24,16},{9,1},{17,9},{25,17},{10,2},{18,10},{26,18},{... | collective-permute-start | bytes 6152 | tf_op jit(solution)/shard_map/ppermute | solution.py:20
  334.2 9.7 %collective-permute-start.18 = (f32[514,1]{1,0:T(8,128)S(1)}, f32[514,1]{1,0:T(8,128)S(1)}, u32[]{:S(2)}, u32[]{:S(2)}) collective-permute-start(f32[514,1]{1,0:T(8,128)S(1)} %get-tuple-element.149), channel_id=1, source_target_pairs={{1,0},{2,1},{3,2},{4,3},{5,4},{6,5},{7,6},{9,8},{10,9},{11,10},{12... | collective-permute-start | bytes 6176 | tf_op jit(solution)/shard_map/ppermute | solution.py:20
  335.5 39.4 %copy-start.4 = (f32[1,4,128,4,128]{4,3,2,1,0:T(4,128)S(1)}, f32[1,4,128,4,128]{4,3,2,1,0:T(4,128)}, u32[]{:S(2)}) copy-start(f32[1,4,128,4,128]{4,3,2,1,0:T(4,128)} %copy-done.2) | copy-start | bytes 3145732
  335.5 15.7 %collective-permute-start.19 = (f32[514,1]{1,0:T(8,128)S(1)}, f32[514,1]{1,0:T(8,128)S(1)}, u32[]{:S(2)}, u32[]{:S(2)}) collective-permute-start(f32[514,1]{1,0:T(8,128)S(1)} %get-tuple-element.150), channel_id=1, source_target_pairs={{0,1},{1,2},{2,3},{3,4},{4,5},{5,6},{6,7},{8,9},{9,10},{10,11},{11... | collective-permute-start | bytes 6176 | tf_op jit(solution)/shard_map/ppermute | solution.py:17
  352.0 3.5 collective-permute-start.21
  354.2 3.1 collective-permute-start.20
  357.4 10.3 %collective-permute-start.22 = (f32[514,1]{1,0:T(8,128)S(1)}, f32[514,1]{1,0:T(8,128)S(1)}, u32[]{:S(2)}, u32[]{:S(2)}) collective-permute-start(f32[514,1]{1,0:T(8,128)S(1)} %get-tuple-element.147), channel_id=1, source_target_pairs={{1,0},{2,1},{3,2},{4,3},{5,4},{6,5},{7,6},{9,8},{10,9},{11,10},{12... | collective-permute-start | bytes 6176 | tf_op jit(solution)/shard_map/ppermute | solution.py:20
  358.7 16.2 %collective-permute-start.23 = (f32[514,1]{1,0:T(8,128)S(1)}, f32[514,1]{1,0:T(8,128)S(1)}, u32[]{:S(2)}, u32[]{:S(2)}) collective-permute-start(f32[514,1]{1,0:T(8,128)S(1)} %get-tuple-element.148), channel_id=1, source_target_pairs={{0,1},{1,2},{2,3},{3,4},{4,5},{5,6},{6,7},{8,9},{9,10},{10,11},{11... | collective-permute-start | bytes 6176 | tf_op jit(solution)/shard_map/ppermute | solution.py:17
where the time goes:
time: 428 us; the launch traced here: 425 us
  blocking collectives  118 us (28%)
  waiting for transfers between devices  109 us (25%)
  starting transfers between devices  70.5 us (16%)
  other arithmetic  66.7 us (16%)
  local copies, waits for them, and re-layouts  26.2 us (6%)
  matrix products  22.6 us (5%)
  between operations  10.6 us (2%)
    psum x3, blocking collectives, two_products(): lax.psum((jnp.sum(current * current), jnp.sum(current * image)), ('row',...  118 us
    ppermute x12, waiting for transfers between devices, extended(): lax.ppermute(lax.slice_in_dim(block, block.shape[dim] - width, None, axis...  43 us
    ppermute x12, starting transfers between devices, extended(): lax.ppermute(lax.slice_in_dim(block, block.shape[dim] - width, None, axis...  40 us
    ppermute x12, waiting for transfers between devices, extended(): lax.ppermute(lax.slice_in_dim(block, 0, width, axis=dim), axis, backward)  39.6 us
    mul x16, other arithmetic, bin_tile(): col_onehot * masked_weight[:, None]  30.8 us
    dot_general x16, matrix products, bin_tile(): lax.dot_general(row_onehot, stacked, (((0,), (0,)), ((), ())), preferred_...  22.6 us
    ppermute x12, starting transfers between devices, extended(): lax.ppermute(lax.slice_in_dim(block, 0, width, axis=dim), axis, backward)  15.5 us
    convert_element_type x16, other arithmetic, bin_tile(): obs_vals.astype(jnp.float32)  14.7 us
  transfers between devices with their start and end apart: 28, of which 22 were waited for; matrix products, arithmetic and copies ran while one was open for 2% of the time, Pallas kernels for 0%

commit v1 on v0

--- a/solution.py
+++ b/solution.py
@@ -7,6 +7,12 @@
 TILE = 128
 ITERS = 3
 smooth_weight = 0.05
+
+
+def flows_manage(s0):
+    raw_out = lax.psum(s0, "col")
+    t1 = lax.psum(raw_out, "row")
+    return t1
 
 
 def extended(block, sides, width):
@@ -93,7 +99,7 @@
     residual = response
 
     def two_products(current, image):
-        return lax.psum((jnp.sum(current * current), jnp.sum(current * image)), ("row", "col"))
+        return flows_manage((jnp.sum(current * current), jnp.sum(current * image)))
 
     image = operate(residual)
     norm_now, curvature = two_products(residual, image)

time: 428 us -> 380 us (0.89)
  blocking collectives: 118 us -> 80 us
  waiting for transfers between devices: 109 us -> 98.8 us
    psum x3 -> x6, blocking collectives: 118 us -> 80 us  [the longest x3 60.8 us: flows_manage(): raw_out = lax.psum(s0, 'col')]
    ppermute x12, waiting for transfers between devices: 43 us -> 37.6 us  [extended(): lax.ppermute(lax.slice_in_dim(block, block.shape[dim] - width, None, axis...]
    ppermute x12, waiting for transfers between devices: 39.6 us -> 35 us  [extended(): lax.ppermute(lax.slice_in_dim(block, 0, width, axis=dim), axis, backward)]
where the time goes in v1:
time: 380 us; the launch traced here: 377 us
  waiting for transfers between devices  98.8 us (26%)
  blocking collectives  80 us (21%)
  starting transfers between devices  71.3 us (19%)
  other arithmetic  66.6 us (18%)
  local copies, waits for them, and re-layouts  26.2 us (7%)
  matrix products  22.6 us (6%)
  between operations  10.8 us (3%)
    psum x3, blocking collectives, flows_manage(): raw_out = lax.psum(s0, 'col')  60.8 us
    ppermute x12, starting transfers between devices, extended(): lax.ppermute(lax.slice_in_dim(block, block.shape[dim] - width, None, axis...  40.7 us
    ppermute x12, waiting for transfers between devices, extended(): lax.ppermute(lax.slice_in_dim(block, block.shape[dim] - width, None, axis...  37.6 us
    ppermute x12, waiting for transfers between devices, extended(): lax.ppermute(lax.slice_in_dim(block, 0, width, axis=dim), axis, backward)  35 us
    mul x16, other arithmetic, bin_tile(): col_onehot * masked_weight[:, None]  30.8 us
    dot_general x16, matrix products, bin_tile(): lax.dot_general(row_onehot, stacked, (((0,), (0,)), ((), ())), preferred_...  22.6 us
    psum x3, blocking collectives, flows_manage(): t1 = lax.psum(raw_out, 'row')  19.2 us
    ppermute x12, starting transfers between devices, extended(): lax.ppermute(lax.slice_in_dim(block, 0, width, axis=dim), axis, backward)  15.5 us
  transfers between devices with their start and end apart: 28, of which 22 were waited for; matrix products, arithmetic and copies ran while one was open for 2% of the time, Pallas kernels for 0%

profile of v1, /device:TPU:0, one launch (start us, length us, event | category | flops | bytes accessed | tf_op | source)
XLA Modules:
  0.0 377.1 jit_solution(11699979559293590564)
XLA Ops:
  2.0 7.3 %all-to-all-start.1 = ((s32[1,16,32]{1,0,2:T(1,128)}), s32[1,16,32]{1,0,2:T(1,128)S(1)}, u32[]{:S(2)}, u32[]{:S(2)}) async-start(s32[1,16,32]{1,0,2:T(1,128)} %copy.16), calls=%async_computation.1 | async-start | bytes 32768 | tf_op jit(solution)/shard_map/all_to_all | solution.py:64
  11.0 5.5 %all-to-all-done.1 = s32[1,16,32]{1,0,2:T(1,128)S(1)} async-done(((s32[1,16,32]{1,0,2:T(1,128)}), s32[1,16,32]{1,0,2:T(1,128)S(1)}, u32[]{:S(2)}, u32[]{:S(2)}) %all-to-all-start.1) | async-done | bytes 2080 | tf_op jit(solution)/shard_map/all_to_all | solution.py:64
  16.4 2.6 all-to-all-start.3
  20.6 1.8 copy.14
  22.5 4.3 %all-to-all-done.3 = bf16[1,16,32,128]{3,1,0,2:T(8,128)(2,1)S(1)} async-done(((bf16[1,16,32,128]{3,1,0,2:T(8,128)(2,1)}), bf16[1,16,32,128]{3,1,0,2:T(8,128)(2,1)S(1)}, u32[]{:S(2)}, u32[]{:S(2)}) %all-to-all-start.3) | async-done | bytes 131104 | tf_op jit(solution)/shard_map/all_to_all | solution.py:67
  26.8 2.6 all-to-all-start.2
  30.3 6.8 %all-to-all-done.2 = bf16[1,16,32,128]{3,1,0,2:T(8,128)(2,1)S(1)} async-done(((bf16[1,16,32,128]{3,1,0,2:T(8,128)(2,1)}), bf16[1,16,32,128]{3,1,0,2:T(8,128)(2,1)S(1)}, u32[]{:S(2)}, u32[]{:S(2)}) %all-to-all-start.2) | async-done | bytes 131104 | tf_op jit(solution)/shard_map/all_to_all | solution.py:68
  37.2 2.6 all-to-all-start
  40.6 9.7 %all-to-all-done = s32[1,16,32,128]{3,1,0,2:T(8,128)S(1)} async-done(((s32[1,16,32,128]{3,1,0,2:T(8,128)}), s32[1,16,32,128]{3,1,0,2:T(8,128)S(1)}, u32[]{:S(2)}, u32[]{:S(2)}) %all-to-all-start) | async-done | bytes 262176 | tf_op jit(solution)/shard_map/all_to_all | solution.py:63
  50.5 83.1 %while.13 = (s32[]{:T(128)}, f32[16,128,256]{2,1,0:T(8,128)S(1)}, s32[16,4096]{1,0:T(8,128)S(1)}, pred[16,4096]{1,0:T(8,128)(4,1)}, bf16[16,4096]{1,0:T(8,128)(2,1)}, /*index=5*/bf16[16,4096]{1,0:T(8,128)(2,1)S(1)}, s32[]{:T(128)}) while((s32[]{:T(128)}, f32[16,128,256]{2,1,0:T(8,128)S(1)}, s32[16,4096]{1,0:T(8,128)S(1)}, ...), condition=%wide.region_1.2_spmd, body=%wide.region_0.1_spmd.sunk | while | flops 274919424 | bytes 4550757 | solution.py:81
  52.3 1.9 fusion.62
  57.5 1.9 fusion.62
  62.7 1.9 fusion.62
  67.9 1.9 fusion.62
  73.1 1.9 fusion.62
  78.3 1.9 fusion.62
  83.5 1.9 fusion.62
  88.7 1.9 fusion.62
  93.9 1.9 fusion.62
  99.0 1.9 fusion.62
  104.2 1.9 fusion.62
  109.4 1.9 fusion.62
  114.6 1.9 fusion.62
  119.8 1.9 fusion.62
  125.0 1.9 fusion.62
  130.2 1.9 fusion.62
  134.9 2.3 reshape.137
  139.9 2.1 collective-permute-start.1
  143.3 2.0 collective-permute-done
  146.7 4.6 %collective-permute-start.3 = (f32[514,1]{1,0:T(8,128)S(1)}, f32[514,1]{1,0:T(8,128)S(1)}, u32[]{:S(2)}, u32[]{:S(2)}) collective-permute-start(f32[514,1]{1,0:T(8,128)S(1)} %get-tuple-element.164), channel_id=1, source_target_pairs={{0,1},{1,2},{2,3},{3,4},{4,5},{5,6},{6,7},{8,9},{9,10},{10,11},{11... | collective-permute-start | bytes 6176 | tf_op jit(solution)/shard_map/ppermute | solution.py:23
  151.3 3.9 %collective-permute-done.2 = f32[514,1]{1,0:T(8,128)S(1)} collective-permute-done((f32[514,1]{1,0:T(8,128)S(1)}, f32[514,1]{1,0:T(8,128)S(1)}, u32[]{:S(2)}, u32[]{:S(2)}) %collective-permute-start.2) | collective-permute-done | bytes 2088 | tf_op jit(solution)/shard_map/ppermute | solution.py:26
  155.2 6.6 %collective-permute-done.3 = f32[514,1]{1,0:T(8,128)S(1)} collective-permute-done((f32[514,1]{1,0:T(8,128)S(1)}, f32[514,1]{1,0:T(8,128)S(1)}, u32[]{:S(2)}, u32[]{:S(2)}) %collective-permute-start.3) | collective-permute-done | bytes 2088 | tf_op jit(solution)/shard_map/ppermute | solution.py:23
  162.5 2.2 collective-permute-start.5
  166.1 1.7 collective-permute-done.4
  169.3 4.8 %collective-permute-start.7 = (f32[514,1]{1,0:T(8,128)S(1)}, f32[514,1]{1,0:T(8,128)S(1)}, u32[]{:S(2)}, u32[]{:S(2)}) collective-permute-start(f32[514,1]{1,0:T(8,128)S(1)} %get-tuple-element.162), channel_id=1, source_target_pairs={{0,1},{1,2},{2,3},{3,4},{4,5},{5,6},{6,7},{8,9},{9,10},{10,11},{11... | collective-permute-start | bytes 6176 | tf_op jit(solution)/shard_map/ppermute | solution.py:23
  174.1 4.1 %collective-permute-done.6 = f32[514,1]{1,0:T(8,128)S(1)} collective-permute-done((f32[514,1]{1,0:T(8,128)S(1)}, f32[514,1]{1,0:T(8,128)S(1)}, u32[]{:S(2)}, u32[]{:S(2)}) %collective-permute-start.6) | collective-permute-done | bytes 2088 | tf_op jit(solution)/shard_map/ppermute | solution.py:26
  178.2 7.2 %collective-permute-done.7 = f32[514,1]{1,0:T(8,128)S(1)} collective-permute-done((f32[514,1]{1,0:T(8,128)S(1)}, f32[514,1]{1,0:T(8,128)S(1)}, u32[]{:S(2)}, u32[]{:S(2)}) %collective-permute-start.7) | collective-permute-done | bytes 2088 | tf_op jit(solution)/shard_map/ppermute | solution.py:23
  185.5 2.6 multiply_reduce_fusion.4
  188.0 20.3 %all-reduce.2 = (f32[]{:T(128)}, f32[]{:T(128)}) all-reduce(f32[]{:T(128)} %get-tuple-element.150, f32[]{:T(128)} %get-tuple-element.140), channel_id=1, replica_groups=mesh['row'=4,'col'=8] {'col'}, use_global_device_ids=true, to_apply=%region_3.4 | all-reduce | flops 2 | bytes 16 | tf_op jit(solution)/shard_map/psum | solution.py:13
  208.3 6.4 %all-reduce.5 = (f32[]{:T(128)}, f32[]{:T(128)}) all-reduce(f32[]{:T(128)} %get-tuple-element.130, f32[]{:T(128)} %get-tuple-element.131), channel_id=1, replica_groups=mesh['row'=4,'col'=8] {'row'}, use_global_device_ids=true, to_apply=%region_4.5 | all-reduce | flops 2 | bytes 16 | tf_op jit(solution)/shard_map/psum | solution.py:14
  220.5 1.7 collective-permute-done.8
  223.7 4.7 %collective-permute-start.11 = (f32[514,1]{1,0:T(8,128)S(1)}, f32[514,1]{1,0:T(8,128)S(1)}, u32[]{:S(2)}, u32[]{:S(2)}) collective-permute-start(f32[514,1]{1,0:T(8,128)S(1)} %get-tuple-element.160), channel_id=1, source_target_pairs={{0,1},{1,2},{2,3},{3,4},{4,5},{5,6},{6,7},{8,9},{9,10},{10,11},{11... | collective-permute-start | bytes 6176 | tf_op jit(solution)/shard_map/ppermute | solution.py:23
  228.4 4.1 %collective-permute-done.10 = f32[514,1]{1,0:T(8,128)S(1)} collective-permute-done((f32[514,1]{1,0:T(8,128)S(1)}, f32[514,1]{1,0:T(8,128)S(1)}, u32[]{:S(2)}, u32[]{:S(2)}) %collective-permute-start.10) | collective-permute-done | bytes 2088 | tf_op jit(solution)/shard_map/ppermute | solution.py:26
  232.5 4.6 %collective-permute-done.11 = f32[514,1]{1,0:T(8,128)S(1)} collective-permute-done((f32[514,1]{1,0:T(8,128)S(1)}, f32[514,1]{1,0:T(8,128)S(1)}, u32[]{:S(2)}, u32[]{:S(2)}) %collective-permute-start.11) | collective-permute-done | bytes 2088 | tf_op jit(solution)/shard_map/ppermute | solution.py:23
  237.9 2.2 collective-permute-start.13
  244.5 5.1 %collective-permute-start.15 = (f32[514,1]{1,0:T(8,128)S(1)}, f32[514,1]{1,0:T(8,128)S(1)}, u32[]{:S(2)}, u32[]{:S(2)}) collective-permute-start(f32[514,1]{1,0:T(8,128)S(1)} %get-tuple-element.158), channel_id=1, source_target_pairs={{0,1},{1,2},{2,3},{3,4},{4,5},{5,6},{6,7},{8,9},{9,10},{10,11},{11... | collective-permute-start | bytes 6176 | tf_op jit(solution)/shard_map/ppermute | solution.py:23
  249.6 3.9 %collective-permute-done.14 = f32[514,1]{1,0:T(8,128)S(1)} collective-permute-done((f32[514,1]{1,0:T(8,128)S(1)}, f32[514,1]{1,0:T(8,128)S(1)}, u32[]{:S(2)}, u32[]{:S(2)}) %collective-permute-start.14) | collective-permute-done | bytes 2088 | tf_op jit(solution)/shard_map/ppermute | solution.py:26
  253.5 7.2 %collective-permute-done.15 = f32[514,1]{1,0:T(8,128)S(1)} collective-permute-done((f32[514,1]{1,0:T(8,128)S(1)}, f32[514,1]{1,0:T(8,128)S(1)}, u32[]{:S(2)}, u32[]{:S(2)}) %collective-permute-start.15) | collective-permute-done | bytes 2088 | tf_op jit(solution)/shard_map/ppermute | solution.py:23
  260.8 2.6 multiply_reduce_fusion.2
  263.4 20.2 %all-reduce.1 = (f32[]{:T(128)}, f32[]{:T(128)}) all-reduce(f32[]{:T(128)} %get-tuple-element.113, f32[]{:T(128)} %get-tuple-element.112), channel_id=1, replica_groups=mesh['row'=4,'col'=8] {'col'}, use_global_device_ids=true, to_apply=%region_9.10 | all-reduce | flops 2 | bytes 16 | tf_op jit(solution)/shard_map/psum | solution.py:13
  283.6 6.4 %all-reduce.4 = (f32[]{:T(128)}, f32[]{:T(128)}) all-reduce(f32[]{:T(128)} %get-tuple-element.128, f32[]{:T(128)} %get-tuple-element.129), channel_id=1, replica_groups=mesh['row'=4,'col'=8] {'row'}, use_global_device_ids=true, to_apply=%region_10.11 | all-reduce | flops 2 | bytes 16 | tf_op jit(solution)/shard_map/psum | solution.py:14
  294.6 1.9 multiply_subtract_fusion.1
  302.7 4.7 %collective-permute-start.19 = (f32[514,1]{1,0:T(8,128)S(1)}, f32[514,1]{1,0:T(8,128)S(1)}, u32[]{:S(2)}, u32[]{:S(2)}) collective-permute-start(f32[514,1]{1,0:T(8,128)S(1)} %get-tuple-element.156), channel_id=1, source_target_pairs={{0,1},{1,2},{2,3},{3,4},{4,5},{5,6},{6,7},{8,9},{9,10},{10,11},{11... | collective-permute-start | bytes 6176 | tf_op jit(solution)/shard_map/ppermute | solution.py:23
  307.4 4.1 %collective-permute-done.18 = f32[514,1]{1,0:T(8,128)S(1)} collective-permute-done((f32[514,1]{1,0:T(8,128)S(1)}, f32[514,1]{1,0:T(8,128)S(1)}, u32[]{:S(2)}, u32[]{:S(2)}) %collective-permute-start.18) | collective-permute-done | bytes 2088 | tf_op jit(solution)/shard_map/ppermute | solution.py:26
  311.5 4.6 %collective-permute-done.19 = f32[514,1]{1,0:T(8,128)S(1)} collective-permute-done((f32[514,1]{1,0:T(8,128)S(1)}, f32[514,1]{1,0:T(8,128)S(1)}, u32[]{:S(2)}, u32[]{:S(2)}) %collective-permute-start.19) | collective-permute-done | bytes 2088 | tf_op jit(solution)/shard_map/ppermute | solution.py:23
  316.9 2.2 collective-permute-start.21
  320.4 1.7 collective-permute-done.20
  323.6 4.9 %collective-permute-start.23 = (f32[514,1]{1,0:T(8,128)S(1)}, f32[514,1]{1,0:T(8,128)S(1)}, u32[]{:S(2)}, u32[]{:S(2)}) collective-permute-start(f32[514,1]{1,0:T(8,128)S(1)} %get-tuple-element.154), channel_id=1, source_target_pairs={{0,1},{1,2},{2,3},{3,4},{4,5},{5,6},{6,7},{8,9},{9,10},{10,11},{11... | collective-permute-start | bytes 6176 | tf_op jit(solution)/shard_map/ppermute | solution.py:23
  328.5 4.1 %collective-permute-done.22 = f32[514,1]{1,0:T(8,128)S(1)} collective-permute-done((f32[514,1]{1,0:T(8,128)S(1)}, f32[514,1]{1,0:T(8,128)S(1)}, u32[]{:S(2)}, u32[]{:S(2)}) %collective-permute-start.22) | collective-permute-done | bytes 2088 | tf_op jit(solution)/shard_map/ppermute | solution.py:26
  332.6 7.2 %collective-permute-done.23 = f32[514,1]{1,0:T(8,128)S(1)} collective-permute-done((f32[514,1]{1,0:T(8,128)S(1)}, f32[514,1]{1,0:T(8,128)S(1)}, u32[]{:S(2)}, u32[]{:S(2)}) %collective-permute-start.23) | collective-permute-done | bytes 2088 | tf_op jit(solution)/shard_map/ppermute | solution.py:23
  339.8 2.5 multiply_reduce_fusion
  342.4 20.3 %all-reduce = (f32[]{:T(128)}, f32[]{:T(128)}) all-reduce(f32[]{:T(128)} %get-tuple-element.111, f32[]{:T(128)} %get-tuple-element.110), channel_id=1, replica_groups=mesh['row'=4,'col'=8] {'col'}, use_global_device_ids=true, to_apply=%region_15.16 | all-reduce | flops 2 | bytes 16 | tf_op jit(solution)/shard_map/psum | solution.py:13
  362.6 6.4 %all-reduce.3 = (f32[]{:T(128)}, f32[]{:T(128)}) all-reduce(f32[]{:T(128)} %get-tuple-element.126, f32[]{:T(128)} %get-tuple-element.127), channel_id=1, replica_groups=mesh['row'=4,'col'=8] {'row'}, use_global_device_ids=true, to_apply=%region_16.17 | all-reduce | flops 2 | bytes 16 | tf_op jit(solution)/shard_map/psum | solution.py:14
  372.8 4.3 %multiply_subtract_fusion = (f32[512,512]{1,0:T(8,128)}, f32[512,512]{1,0:T(8,128)}) fusion(f32[512,512]{1,0:T(8,128)S(1)} %multiply_subtract_fusion.1, f32[512,512]{1,0:T(8,128)} %get-tuple-element.138, f32[]{:T(128)S(6)} %div.37, f32[]{:T(128)S(6)} %div.39, f32[512,512]{1,0:T(8,128)} %get-tuple-element.139, f32[512,512]{1,0:T(8,128)} %get-tuple-element.141, ...), kind=kLoop, calls=%fused_computation.118 | loop fusion | flops 3932160 | bytes 8388628 | tf_op jit(solution)/shard_map/sub | solution.py:110
  (162 shorter events, 88.9 us)
Async XLA Ops:
  2.0 14.4 %all-to-all-start.1 = ((s32[1,16,32]{1,0,2:T(1,128)}), s32[1,16,32]{1,0,2:T(1,128)S(1)}, u32[]{:S(2)}, u32[]{:S(2)}) async-start(s32[1,16,32]{1,0,2:T(1,128)} %copy.16), calls=%async_computation.1 | async-start | bytes 32768 | tf_op jit(solution)/shard_map/all_to_all | solution.py:64
  16.4 10.4 %all-to-all-start.3 = ((bf16[1,16,32,128]{3,1,0,2:T(8,128)(2,1)}), bf16[1,16,32,128]{3,1,0,2:T(8,128)(2,1)S(1)}, u32[]{:S(2)}, u32[]{:S(2)}) async-start(bf16[1,16,32,128]{3,1,0,2:T(8,128)(2,1)} %copy.20), calls=%async_computation.3 | async-start | bytes 262144 | tf_op jit(solution)/shard_map/all_to_all | solution.py:67
  26.8 10.4 %all-to-all-start.2 = ((bf16[1,16,32,128]{3,1,0,2:T(8,128)(2,1)}), bf16[1,16,32,128]{3,1,0,2:T(8,128)(2,1)S(1)}, u32[]{:S(2)}, u32[]{:S(2)}) async-start(bf16[1,16,32,128]{3,1,0,2:T(8,128)(2,1)} %copy.18), calls=%async_computation.2 | async-start | bytes 262144 | tf_op jit(solution)/shard_map/all_to_all | solution.py:68
  37.2 13.0 %all-to-all-start = ((s32[1,16,32,128]{3,1,0,2:T(8,128)}), s32[1,16,32,128]{3,1,0,2:T(8,128)S(1)}, u32[]{:S(2)}, u32[]{:S(2)}) async-start(s32[1,16,32,128]{3,1,0,2:T(8,128)} %copy.14), calls=%async_computation | async-start | bytes 524288 | tf_op jit(solution)/shard_map/all_to_all | solution.py:63
  133.6 1.3 copy-start.5
  139.8 45.7 %copy-start.2 = (f32[1,4,128,4,128]{4,3,2,1,0:T(4,128)}, f32[1,4,128,4,128]{4,3,2,1,0:T(4,128)S(1)}, u32[]{:S(2)}) copy-start(f32[1,4,128,4,128]{4,3,2,1,0:T(4,128)S(1)} %get-tuple-element.151) | copy-start | bytes 3145732
  139.8 76.2 %copy-start.1 = (f32[1,4,128,4,128]{4,3,2,1,0:T(4,128)}, f32[1,4,128,4,128]{4,3,2,1,0:T(4,128)S(1)}, u32[]{:S(2)}) copy-start(f32[1,4,128,4,128]{4,3,2,1,0:T(4,128)S(1)} %get-tuple-element.152) | copy-start | bytes 3145732
  139.8 22.0 %copy-start = (f32[512,512]{1,0:T(8,128)S(1)}, f32[512,512]{1,0:T(8,128)}, u32[]{:S(2)}) copy-start(f32[512,512]{1,0:T(8,128)} %param.11) | copy-start | bytes 3145732
  139.9 3.4 collective-permute-start.1
  142.0 3.3 collective-permute-start
  145.4 9.8 %collective-permute-start.2 = (f32[514,1]{1,0:T(8,128)S(1)}, f32[514,1]{1,0:T(8,128)S(1)}, u32[]{:S(2)}, u32[]{:S(2)}) collective-permute-start(f32[514,1]{1,0:T(8,128)S(1)} %get-tuple-element.163), channel_id=1, source_target_pairs={{1,0},{2,1},{3,2},{4,3},{5,4},{6,5},{7,6},{9,8},{10,9},{11,10},{12... | collective-permute-start | bytes 6176 | tf_op jit(solution)/shard_map/ppermute | solution.py:26
  146.7 15.1 %collective-permute-start.3 = (f32[514,1]{1,0:T(8,128)S(1)}, f32[514,1]{1,0:T(8,128)S(1)}, u32[]{:S(2)}, u32[]{:S(2)}) collective-permute-start(f32[514,1]{1,0:T(8,128)S(1)} %get-tuple-element.164), channel_id=1, source_target_pairs={{0,1},{1,2},{2,3},{3,4},{4,5},{5,6},{6,7},{8,9},{9,10},{10,11},{11... | collective-permute-start | bytes 6176 | tf_op jit(solution)/shard_map/ppermute | solution.py:23
  162.5 3.5 collective-permute-start.5
  164.8 3.1 collective-permute-start.4
  168.0 10.3 %collective-permute-start.6 = (f32[514,1]{1,0:T(8,128)S(1)}, f32[514,1]{1,0:T(8,128)S(1)}, u32[]{:S(2)}, u32[]{:S(2)}) collective-permute-start(f32[514,1]{1,0:T(8,128)S(1)} %get-tuple-element.161), channel_id=1, source_target_pairs={{1,0},{2,1},{3,2},{4,3},{5,4},{6,5},{7,6},{9,8},{10,9},{11,10},{12... | collective-permute-start | bytes 6176 | tf_op jit(solution)/shard_map/ppermute | solution.py:26
  169.3 16.2 %collective-permute-start.7 = (f32[514,1]{1,0:T(8,128)S(1)}, f32[514,1]{1,0:T(8,128)S(1)}, u32[]{:S(2)}, u32[]{:S(2)}) collective-permute-start(f32[514,1]{1,0:T(8,128)S(1)} %get-tuple-element.162), channel_id=1, source_target_pairs={{0,1},{1,2},{2,3},{3,4},{4,5},{5,6},{6,7},{8,9},{9,10},{10,11},{11... | collective-permute-start | bytes 6176 | tf_op jit(solution)/shard_map/ppermute | solution.py:23
  217.5 3.0 collective-permute-start.9
  219.1 3.1 collective-permute-start.8
  222.3 10.1 %collective-permute-start.10 = (f32[514,1]{1,0:T(8,128)S(1)}, f32[514,1]{1,0:T(8,128)S(1)}, u32[]{:S(2)}, u32[]{:S(2)}) collective-permute-start(f32[514,1]{1,0:T(8,128)S(1)} %get-tuple-element.159), channel_id=1, source_target_pairs={{1,0},{2,1},{3,2},{4,3},{5,4},{6,5},{7,6},{9,8},{10,9},{11,10},{12... | collective-permute-start | bytes 6176 | tf_op jit(solution)/shard_map/ppermute | solution.py:26
  223.7 37.1 %copy-start.3 = (f32[1,4,128,4,128]{4,3,2,1,0:T(4,128)S(1)}, f32[1,4,128,4,128]{4,3,2,1,0:T(4,128)}, u32[]{:S(2)}) copy-start(f32[1,4,128,4,128]{4,3,2,1,0:T(4,128)} %copy-done.2) | copy-start | bytes 3145732
  223.7 13.4 %collective-permute-start.11 = (f32[514,1]{1,0:T(8,128)S(1)}, f32[514,1]{1,0:T(8,128)S(1)}, u32[]{:S(2)}, u32[]{:S(2)}) collective-permute-start(f32[514,1]{1,0:T(8,128)S(1)} %get-tuple-element.160), channel_id=1, source_target_pairs={{0,1},{1,2},{2,3},{3,4},{4,5},{5,6},{6,7},{8,9},{9,10},{10,11},{11... | collective-permute-start | bytes 6176 | tf_op jit(solution)/shard_map/ppermute | solution.py:23
  237.9 3.5 collective-permute-start.13
  240.0 3.1 collective-permute-start.12
  243.2 10.3 %collective-permute-start.14 = (f32[514,1]{1,0:T(8,128)S(1)}, f32[514,1]{1,0:T(8,128)S(1)}, u32[]{:S(2)}, u32[]{:S(2)}) collective-permute-start(f32[514,1]{1,0:T(8,128)S(1)} %get-tuple-element.157), channel_id=1, source_target_pairs={{1,0},{2,1},{3,2},{4,3},{5,4},{6,5},{7,6},{9,8},{10,9},{11,10},{12... | collective-permute-start | bytes 6176 | tf_op jit(solution)/shard_map/ppermute | solution.py:26
  244.5 16.2 %collective-permute-start.15 = (f32[514,1]{1,0:T(8,128)S(1)}, f32[514,1]{1,0:T(8,128)S(1)}, u32[]{:S(2)}, u32[]{:S(2)}) collective-permute-start(f32[514,1]{1,0:T(8,128)S(1)} %get-tuple-element.158), channel_id=1, source_target_pairs={{0,1},{1,2},{2,3},{3,4},{4,5},{5,6},{6,7},{8,9},{9,10},{10,11},{11... | collective-permute-start | bytes 6176 | tf_op jit(solution)/shard_map/ppermute | solution.py:23
  296.5 3.0 collective-permute-start.17
  298.2 3.1 collective-permute-start.16
  301.4 10.1 %collective-permute-start.18 = (f32[514,1]{1,0:T(8,128)S(1)}, f32[514,1]{1,0:T(8,128)S(1)}, u32[]{:S(2)}, u32[]{:S(2)}) collective-permute-start(f32[514,1]{1,0:T(8,128)S(1)} %get-tuple-element.155), channel_id=1, source_target_pairs={{1,0},{2,1},{3,2},{4,3},{5,4},{6,5},{7,6},{9,8},{10,9},{11,10},{12... | collective-permute-start | bytes 6176 | tf_op jit(solution)/shard_map/ppermute | solution.py:26
  302.7 37.1 %copy-start.4 = (f32[1,4,128,4,128]{4,3,2,1,0:T(4,128)S(1)}, f32[1,4,128,4,128]{4,3,2,1,0:T(4,128)}, u32[]{:S(2)}) copy-start(f32[1,4,128,4,128]{4,3,2,1,0:T(4,128)} %copy-done.2) | copy-start | bytes 3145732
  302.7 13.4 %collective-permute-start.19 = (f32[514,1]{1,0:T(8,128)S(1)}, f32[514,1]{1,0:T(8,128)S(1)}, u32[]{:S(2)}, u32[]{:S(2)}) collective-permute-start(f32[514,1]{1,0:T(8,128)S(1)} %get-tuple-element.156), channel_id=1, source_target_pairs={{0,1},{1,2},{2,3},{3,4},{4,5},{5,6},{6,7},{8,9},{9,10},{10,11},{11... | collective-permute-start | bytes 6176 | tf_op jit(solution)/shard_map/ppermute | solution.py:23
  316.9 3.5 collective-permute-start.21
  319.1 3.1 collective-permute-start.20
  322.3 10.3 %collective-permute-start.22 = (f32[514,1]{1,0:T(8,128)S(1)}, f32[514,1]{1,0:T(8,128)S(1)}, u32[]{:S(2)}, u32[]{:S(2)}) collective-permute-start(f32[514,1]{1,0:T(8,128)S(1)} %get-tuple-element.153), channel_id=1, source_target_pairs={{1,0},{2,1},{3,2},{4,3},{5,4},{6,5},{7,6},{9,8},{10,9},{11,10},{12... | collective-permute-start | bytes 6176 | tf_op jit(solution)/shard_map/ppermute | solution.py:26
  323.6 16.2 %collective-permute-start.23 = (f32[514,1]{1,0:T(8,128)S(1)}, f32[514,1]{1,0:T(8,128)S(1)}, u32[]{:S(2)}, u32[]{:S(2)}) collective-permute-start(f32[514,1]{1,0:T(8,128)S(1)} %get-tuple-element.154), channel_id=1, source_target_pairs={{0,1},{1,2},{2,3},{3,4},{4,5},{5,6},{6,7},{8,9},{9,10},{10,11},{11... | collective-permute-start | bytes 6176 | tf_op jit(solution)/shard_map/ppermute | solution.py:23
